TPU v7x, 32 devices: a whole 2x2x4 slice. The times are simulated.
32 devices in a mesh: row: 8 (over z, core), col: 4 (over y, x).
Axes of the slice: x: 2, y: 2, z: 4, core: 2. Of those that a mesh axis runs over, the one named last changes fastest.
Arguments:
- genotypes: int32 [512, 16384], P(('row', 'col')), may hold values from 0 to 2, as said below
- snp_index: int32 [512], P(('row', 'col')), may hold values from 0 to 2047, as said below
- freq_table: float32 [2048], replicated, as said below
- prior: float32 [16384, 16384], P('row', 'col'), as said below
- start_vectors: float32 [16384, 20], P('row'), may hold values from -6 to 6
Outputs:
- grm: float32 [16384, 16384], P('row', 'col')
- pcs: float32 [16384, 20], P('col')
- spectrum: float32 [3, 20], replicated
Inputs may be any that keep to these rules, and one draw needn't show every extreme that they name: `genotypes`: genotype dosages 0, 1 or 2. `snp_index`: strictly increasing; entry j lies in 4 * j to 4 * j + 3. `freq_table`: frequencies are multiples of 1/1024 between 52/1024 and 512/1024. `prior`: exactly symmetric; diagonal between 1 and 2, off-diagonal entries small.
All inputs are finite; a program needn't handle non-finite values.
Results may differ from a plain program's by a relative error of at most 0.0075.
Values may be sent and summed in bfloat16 or wider, within the bound.
A program may use at most 128 MiB of HBM per device.

v0:
```python
import jax
import jax.numpy as jnp
from jax import lax
from jax.sharding import PartitionSpec as P

S = 16384
ITERS = 3


def standardize(genotypes, allele_freq):
    doubled = 2.0 * allele_freq
    spread = jnp.sqrt(doubled * (1.0 - allele_freq))
    return (genotypes.astype(jnp.float32) - doubled[:, None]) / spread[:, None]


def orthonormal(factor, image):
    return lax.linalg.triangular_solve(factor, image, left_side=False, lower=True, transpose_a=True)


def apply_tile(tile, vectors, transposed):
    if transposed:
        return lax.dot_general(
            tile, vectors, (((0,), (0,)), ((), ())), precision=lax.Precision.HIGHEST
        )
    return jnp.dot(tile, vectors, precision=lax.Precision.HIGHEST)


def local_gram(image):
    return jnp.dot(image.T, image, precision=lax.Precision.HIGHEST)


def body(genotypes, snp_index, freq_table, prior, start_vectors):
    allele_freq = jnp.take(freq_table, snp_index)
    standard = standardize(genotypes, allele_freq).astype(jnp.bfloat16)
    row_count = lax.axis_size("row")
    col_count = lax.axis_size("col")
    own_snps = genotypes.shape[0]
    total_snps = own_snps * row_count * col_count
    row_piece = lax.all_to_all(standard, "row", split_axis=1, concat_axis=0, tiled=True)
    col_piece = lax.all_to_all(standard, "col", split_axis=1, concat_axis=0, tiled=True)
    col_piece = col_piece.reshape(col_count, 1, own_snps, col_piece.shape[1])
    col_panel = lax.all_gather(col_piece, "row", axis=1, tiled=True)
    col_panel = col_panel.reshape(total_snps, col_panel.shape[3])
    window = lax.dot_general(
        lax.all_gather(row_piece, "col", axis=0, tiled=True),
        col_panel,
        (((0,), (0,)), ((), ())),
        preferred_element_type=jnp.float32,
    )
    grm = prior + window / total_snps
    scaled_start = start_vectors / jnp.sqrt(jnp.float32(S))
    diagonals = []
    image = lax.psum(apply_tile(grm, scaled_start, True), "row")
    for step in range(1, ITERS):
        if step % 2 == 1:
            product, gram = lax.psum((apply_tile(grm, image, False), local_gram(image)), "col")
        else:
            product, gram = lax.psum((apply_tile(grm, image, True), local_gram(image)), "row")
        factor = jnp.linalg.cholesky(gram)
        diagonals.append(jnp.diagonal(factor))
        image = orthonormal(factor, product)
    gram = lax.psum(local_gram(image), "col")
    factor = jnp.linalg.cholesky(gram)
    diagonals.append(jnp.diagonal(factor))
    vectors = orthonormal(factor, image)
    pcs = vectors * jnp.sqrt(jnp.float32(S))
    spectrum = jnp.stack(diagonals, axis=0)
    return (grm, pcs, spectrum)


def solution(mesh):
    return jax.shard_map(
        body,
        mesh=mesh,
        in_specs=(P(("row", "col"), None), P(("row", "col")), P(), P("row", "col"), P("row", None)),
        out_specs=(P("row", "col"), P("col", None), P()),
        check_vma=False,
    )
```

profile of v0, /device:TPU:0, one launch (start us, length us, event | category | flops | bytes accessed | tf_op | source)
XLA Modules:
  0.0 454.8 jit_solution(4961095967382614033)
XLA Ops:
  7.2 0.7 compare_select_fusion
  7.9 0.7 gather_fusion
  8.6 0.7 broadcast_multiply_fusion
  9.2 1.4 divide_convert_fusion
  10.7 13.5 %all_to_all.35 = bf16[16,4,4096]{2,0,1:T(8,128)(2,1)S(1)} all-to-all(bf16[16,4,4096]{2,0,1:T(8,128)(2,1)S(1)} %bitcast.73), channel_id=1, replica_groups=mesh['row'=8,'col'=4] {'col'}, dimensions={1} | all-to-all | bytes 1048576 | tf_op jit(solution)/shard_map/all_to_all | solution.py:40
  24.2 1.2 copy.30
  25.4 0.0 all-gather.4.cloned.1.call-start
  25.5 31.8 %all_to_all.36 = bf16[16,8,2048]{2,0,1:T(8,128)(2,1)} all-to-all(bf16[16,8,2048]{2,0,1:T(8,128)(2,1)S(1)} %bitcast.72), channel_id=1, replica_groups=mesh['row'=8,'col'=4] {'row'}, dimensions={1} | all-to-all | bytes 1048576 | tf_op jit(solution)/shard_map/all_to_all | solution.py:39
  57.3 0.0 all-reduce.4.cloned.1.call-start
  57.4 23.7 %all-gather.6.cloned.1.call-done = bf16[4,128,4096]{2,0,1:T(4,128)(2,1)} async-done(((bf16[4,16,4096]{2,0,1:T(4,128)(2,1)}), bf16[4,128,4096]{2,0,1:T(4,128)(2,1)}) %all-gather.6.cloned.1.call-update) | async-done | bytes 4194320 | tf_op jit(solution)/shard_map/all_gather | solution.py:42
  81.1 6.5 %copy.31 = bf16[4,128,4096]{2,1,0:T(8,128)(2,1)} copy(bf16[4,128,4096]{2,0,1:T(4,128)(2,1)} %all-gather.6.cloned.1.call-done) | data formatting | bytes 8388608 | tf_op jit(solution)/shard_map/all_gather | solution.py:42
  87.5 28.0 %all-gather.4.cloned.1.call-done = bf16[512,2048]{1,0:T(8,128)(2,1)} async-done(((bf16[128,2048]{1,0:T(8,128)(2,1)}), bf16[512,2048]{1,0:T(8,128)(2,1)}) %all-gather.4.cloned.1.call-update) | async-done | bytes 2097168 | tf_op jit(solution)/shard_map/all_gather | solution.py:45
  115.5 28.8 %multiply_add_fusion = f32[2048,4096]{1,0:T(8,128)} fusion(f32[2048,4096]{1,0:T(8,128)} %param.11, bf16[512,2048]{1,0:T(8,128)(2,1)} %all-gather.4.cloned.1.call-done, bf16[512,4096]{1,0:T(8,128)(2,1)} %bitcast.67), kind=kOutput, calls=%fused_computation.4 | convolution fusion | flops 8606711808 | bytes 73400320 | tf_op jit(solution)/shard_map/dot_general | solution.py:44
  144.3 22.0 %fusion.1 = f32[4096,20]{0,1:T(8,128)} fusion(f32[2048,4096]{1,0:T(8,128)} %multiply_add_fusion, f32[2048,20]{0,1:T(8,128)S(1)} %copy-done.2), kind=kOutput, calls=%fused_computation.11 | convolution fusion | flops 2013306880 | bytes 34045952 | tf_op jit(solution)/shard_map/dot_general | solution.py:22
  166.4 0.0 all-reduce.6.cloned.1.call-start
  166.4 55.9 %all-reduce.4.cloned.1.call-done = f32[4096,20]{0,1:T(8,128)} async-done(((f32[4096,20]{0,1:T(8,128)}), f32[4096,20]{0,1:T(8,128)}) %all-reduce.4.cloned.1.call-update) | async-done | bytes 327696 | tf_op jit(solution)/shard_map/psum | solution.py:53
  222.4 1.6 fusion.27
  224.0 15.9 %psum.44 = f32[20,20]{0,1:T(8,128)S(1)} all-reduce(f32[20,20]{0,1:T(8,128)S(1)} %fusion.27), channel_id=1, replica_groups=mesh['row'=8,'col'=4] {'col'}, use_global_device_ids=true, to_apply=%region_2.3 | all-reduce | flops 400 | bytes 3200 | tf_op jit(solution)/shard_map/psum | solution.py:56
  239.9 0.1 copy.33
  240.0 1.8 cholesky.59
  241.9 0.6 compare_reduce_fusion.2
  242.5 32.6 %fusion.26 = f32[2048,20]{0,1:T(8,128)} fusion(f32[2048,4096]{1,0:T(8,128)} %multiply_add_fusion, f32[4096,20]{0,1:T(8,128)} %all-reduce.4.cloned.1.call-done), kind=kOutput, calls=%fused_computation.50 | convolution fusion | flops 2013265920 | bytes 34045952 | tf_op jit(solution)/shard_map/dot_general | solution.py:25
  275.2 0.7 fusion.17
  275.9 1.5 custom-call.8
  277.4 0.8 gather_fusion.1
  278.2 37.0 %all-reduce.6.cloned.1.call-done = f32[2048,20]{0,1:T(8,128)} async-done(((f32[2048,20]{0,1:T(8,128)}), f32[2048,20]{0,1:T(8,128)}) %all-reduce.6.cloned.1.call-update) | async-done | bytes 163856 | tf_op jit(solution)/shard_map/psum | solution.py:56
  315.2 1.3 fusion.8
  316.5 0.3 fusion.28
  316.8 22.0 %fusion.29 = f32[4096,20]{0,1:T(8,128)} fusion(f32[2048,4096]{1,0:T(8,128)} %multiply_add_fusion, f32[2048,20]{0,1:T(8,128)S(1)} %fusion.8), kind=kOutput, calls=%fused_computation.53 | convolution fusion | flops 2013265920 | bytes 34045952 | tf_op jit(solution)/shard_map/dot_general | solution.py:22
  338.8 28.1 %psum.45 = f32[20,20]{0,1:T(8,128)S(1)} all-reduce(f32[20,20]{0,1:T(8,128)S(1)} %fusion.28), channel_id=1, replica_groups=mesh['row'=8,'col'=4] {'row'}, use_global_device_ids=true, to_apply=%region_5.7 | all-reduce | flops 400 | bytes 3200 | tf_op jit(solution)/shard_map/psum | solution.py:58
  366.9 0.1 copy.35
  367.0 1.8 cholesky.70
  368.8 0.6 compare_reduce_fusion.1
  369.5 0.7 fusion.16
  370.1 1.5 custom-call.16
  371.7 0.8 gather_fusion.2
  372.5 50.4 %all-reduce.8.cloned.1.call-done = f32[4096,20]{0,1:T(8,128)} async-done(((f32[4096,20]{0,1:T(8,128)}), f32[4096,20]{0,1:T(8,128)}) %all-reduce.8.cloned.1.call-update) | async-done | bytes 327696 | tf_op jit(solution)/shard_map/psum | solution.py:58
  422.9 1.5 convolution_bitcast_fusion.1
  424.4 0.5 fusion.30
  424.9 15.9 %psum.47 = f32[20,20]{0,1:T(8,128)S(1)} all-reduce(f32[20,20]{0,1:T(8,128)S(1)} %fusion.30), channel_id=1, replica_groups=mesh['row'=8,'col'=4] {'col'}, use_global_device_ids=true, to_apply=%region_7.10 | all-reduce | flops 400 | bytes 3200 | tf_op jit(solution)/shard_map/psum | solution.py:62
  440.8 0.1 copy.37
  441.0 1.8 cholesky.81
  442.8 0.6 compare_reduce_fusion
  443.4 0.7 select_bitcast_fusion
  444.1 0.8 gather_fusion.3
  444.9 1.5 custom-call.17
  446.4 1.3 fusion
  447.7 0.6 pad_maximum_fusion
  (24 shorter events, 0.4 us)
Async XLA Ops:
  7.2 0.7 copy-start
  7.2 73.9 %all-gather.6.cloned.1.call-start = ((), (), s32[]{:S(2)}) async-start(), calls=%async_computation.6 | async-start | bytes 4718592 | tf_op jit(solution)/shard_map/all_gather | solution.py:42
  25.4 90.0 %all-gather.4.cloned.1.call-start = ((), (), s32[]{:S(2)}) async-start(), calls=%async_computation.2 | async-start | bytes 2621440 | tf_op jit(solution)/shard_map/all_gather | solution.py:45
  57.3 165.1 %all-reduce.4.cloned.1.call-start = ((), (), s32[]{:S(2)}) async-start(), calls=%async_computation.3 | async-start | bytes 786432 | tf_op jit(solution)/shard_map/psum | solution.py:53
  115.5 28.8 %copy-start.2 = (f32[2048,20]{0,1:T(8,128)S(1)}, f32[2048,20]{0,1:T(8,128)}, u32[]{:S(2)}) copy-start(f32[2048,20]{0,1:T(8,128)} %param.12) | copy-start | bytes 491524
  166.4 148.8 %all-reduce.6.cloned.1.call-start = ((), (), s32[]{:S(2)}) async-start(), calls=%async_computation.4 | async-start | bytes 393216 | tf_op jit(solution)/shard_map/psum | solution.py:56
  242.5 205.8 %copy-start.1 = (f32[2048]{0:T(1024)S(1)}, f32[2048]{0:T(1024)}, u32[]{:S(2)}) copy-start(f32[2048]{0:T(1024)} %param.10) | copy-start | bytes 24580
  275.2 147.7 %all-reduce.8.cloned.1.call-start = ((), (), s32[]{:S(2)}) async-start(), calls=%async_computation.5 | async-start | bytes 786432 | tf_op jit(solution)/shard_map/psum | solution.py:58
Sparse Core Ops, SparseCore 0:
  25.5 55.4 all-gather.5
  82.9 32.5 all-gather.3
  166.5 55.8 all-reduce.3
  275.3 39.8 all-reduce.5
  369.6 53.2 all-reduce.7
where the time goes:
time: 455 us
  waiting for transfers between devices  195 us (43%)
  matrix products  112 us (25%)
  blocking collectives  105 us (23%)
  other arithmetic  17.4 us (4%)
  between operations  13.9 us (3%)
  local copies, waits for them, and re-layouts  11.1 us (2%)
    psum x1, waiting for transfers between devices, body(): image = lax.psum(apply_tile(grm, scaled_start, True), 'row')  55.9 us
    psum x1, waiting for transfers between devices, body(): lax.psum((apply_tile(grm, image, True), local_gram(image)), 'row')  50.4 us
    dot_general x2, matrix products, apply_tile(): lax.dot_general(tile, vectors, (((0,), (0,)), ((), ())), precision=lax.Pr...  44.1 us
    psum x1, waiting for transfers between devices, body(): lax.psum((apply_tile(grm, image, False), local_gram(image)), 'col')  37 us
    dot_general x1, matrix products, apply_tile(): return jnp.dot(tile, vectors, precision=lax.Precision.HIGHEST)  32.6 us
    all_to_all x1, blocking collectives, body(): lax.all_to_all(standard, 'row', split_axis=1, concat_axis=0, tiled=True)  31.8 us
    dot_general x1, matrix products, body(): lax.dot_general(lax.all_gather(row_piece, 'col', axis=0, tiled=True), col...  28.8 us
    psum x1, blocking collectives, body(): lax.psum((apply_tile(grm, image, True), local_gram(image)), 'row')  28.1 us
  transfers between devices with their start and end apart: 5, of which 5 were waited for; matrix products, arithmetic and copies ran while one was open for 3% of the time, Pallas kernels for 0%

commit v1 on v0

v1 whole, which is shorter than its diff:
```python
import functools

import jax
import jax.numpy as jnp
from jax import lax
from jax.experimental import pallas as pl
from jax.experimental.pallas import tpu as pltpu
from jax.sharding import PartitionSpec as P

ITERS = 3
MESH = pl.DeviceIdType.MESH


def standardize(genotypes, allele_freq):
    doubled = 2.0 * allele_freq
    spread = jnp.sqrt(doubled * (1.0 - allele_freq))
    return (genotypes.astype(jnp.float32) - doubled[:, None]) / spread[:, None]


def tile_kernel(scale, rows_ref, cols_ref, prior_ref, grm_ref, short_ref, turned):
    @pl.when(pl.program_id(1) == 0)
    def _():
        turned[...] = rows_ref[...].T

    window = jnp.dot(turned[...], cols_ref[...], preferred_element_type=jnp.float32)
    grm = prior_ref[...] + window * scale
    grm_ref[...] = grm
    short_ref[...] = grm.astype(jnp.bfloat16)


def make_tile(row_panel, col_panel, prior):
    depth = row_panel.shape[0]
    rows, cols = prior.shape
    bm, bn = min(512, rows), min(1024, cols)
    return pl.pallas_call(
        functools.partial(tile_kernel, 1.0 / depth),
        grid=(rows // bm, cols // bn),
        in_specs=[
            pl.BlockSpec((depth, bm), lambda i, j: (0, i)),
            pl.BlockSpec((depth, bn), lambda i, j: (0, j)),
            pl.BlockSpec((bm, bn), lambda i, j: (i, j)),
        ],
        out_specs=[
            pl.BlockSpec((bm, bn), lambda i, j: (i, j)),
            pl.BlockSpec((bm, bn), lambda i, j: (i, j)),
        ],
        out_shape=[
            jax.ShapeDtypeStruct((rows, cols), jnp.float32),
            jax.ShapeDtypeStruct((rows, cols), jnp.bfloat16),
        ],
        scratch_shapes=[pltpu.VMEM((bm, depth), jnp.bfloat16)],
        compiler_params=pltpu.CompilerParams(
            dimension_semantics=("arbitrary", "arbitrary"),
            vmem_limit_bytes=56 * 2**20,
        ),
        cost_estimate=pl.CostEstimate(
            flops=2 * rows * cols * depth, bytes_accessed=10 * rows * cols, transcendentals=0
        ),
        name="tile",
    )(row_panel, col_panel, prior)


def sum_kernel(axis, n, with_block, with_gram, *refs):
    refs = list(refs)
    x_ref = refs.pop(0) if with_block else None
    g_ref = refs.pop(0) if with_gram else None
    y_ref = refs.pop(0) if with_block else None
    h_ref = refs.pop(0) if with_gram else None
    if with_block:
        parts, own, land, s1, r1, s2, r2 = refs[:7]
        refs = refs[7:]
    if with_gram:
        grams, s3, r3 = refs
    me = lax.axis_index(axis)
    peers = [lax.rem(me + d, n) for d in range(1, n)]

    barrier = pltpu.get_barrier_semaphore()
    for peer in peers:
        pl.semaphore_signal(barrier, inc=1, device_id={axis: peer}, device_id_type=MESH)
    pl.semaphore_wait(barrier, n - 1)

    def send(src, dst, send_sem, recv_sem, peer):
        copy = pltpu.make_async_remote_copy(
            src_ref=src,
            dst_ref=dst,
            send_sem=send_sem,
            recv_sem=recv_sem,
            device_id={axis: peer},
            device_id_type=MESH,
        )
        copy.start()
        return copy

    first, second, third = [], [], []
    if with_block:
        for d, peer in enumerate(peers):
            first.append(send(x_ref.at[peer], parts.at[d], s1.at[d], r1.at[d], peer))
    if with_gram:
        for d, peer in enumerate(peers):
            third.append(send(g_ref, grams.at[me], s3.at[d], r3.at[d], peer))
        grams[me] = g_ref[...]
    if with_block:
        total = x_ref[me].astype(jnp.float32)
        for d, copy in enumerate(first):
            copy.wait_recv()
            total = total + parts[d].astype(jnp.float32)
        own[...] = total.astype(jnp.bfloat16)
        for d, peer in enumerate(peers):
            second.append(send(own, land.at[me], s2.at[d], r2.at[d], peer))
        land[me] = total.astype(jnp.bfloat16)
    if with_gram:
        for copy in third:
            copy.wait_recv()
        gram = grams[0]
        for j in range(1, n):
            gram = gram + grams[j]
        h_ref[...] = gram
    if with_block:
        for copy in second:
            copy.wait_recv()
        length = land.shape[2]
        for j in range(n):
            y_ref[:, j * length : (j + 1) * length] = land[j]
    for copy in first + second + third:
        copy.wait_send()


def axis_sum(axis, ident, block=None, gram=None):
    n = lax.axis_size(axis)
    dma = pltpu.SemaphoreType.DMA
    args, outs, scratch = [], [], []
    if block is not None:
        height, width = block.shape
        length = width // n
        args.append(block.reshape(height, n, length).transpose(1, 0, 2))
        outs.append(jax.ShapeDtypeStruct((height, width), jnp.bfloat16))
        scratch += [
            pltpu.VMEM((n - 1, height, length), jnp.bfloat16),
            pltpu.VMEM((height, length), jnp.bfloat16),
            pltpu.VMEM((n, height, length), jnp.bfloat16),
        ] + [dma((n - 1,))] * 4
    if gram is not None:
        args.append(gram)
        outs.append(jax.ShapeDtypeStruct(gram.shape, jnp.float32))
        scratch += [pltpu.VMEM((n,) + gram.shape, jnp.float32)] + [dma((n - 1,))] * 2
    vmem = pl.BlockSpec(memory_space=pltpu.VMEM)
    return pl.pallas_call(
        functools.partial(sum_kernel, axis, n, block is not None, gram is not None),
        in_specs=[vmem] * len(args),
        out_specs=[vmem] * len(outs),
        out_shape=outs,
        scratch_shapes=scratch,
        compiler_params=pltpu.CompilerParams(collective_id=ident, has_side_effects=True),
        name="sum" + str(ident),
    )(*args)


def factor_kernel(count, gain, gram_ref, block_ref, out_ref, diag_ref):
    height = gram_ref.shape[0]
    row = lax.broadcasted_iota(jnp.int32, (height, height), 0)
    col = lax.broadcasted_iota(jnp.int32, (height, height), 1)
    gram = gram_ref[...]
    inverse = jnp.where(row == col, 1.0, 0.0).astype(jnp.float32)
    diag = jnp.zeros((height, height), jnp.float32)
    for k in range(count):
        pivot = gram[k : k + 1, k : k + 1]
        root = jnp.sqrt(pivot)
        diag = jnp.where((row == 0) & (col == k), root, diag)
        head = gram[k : k + 1, :] / root
        tail = inverse[k : k + 1, :] / root
        below = jnp.where(row[:, :1] > k, gram[:, k : k + 1] / root, 0.0)
        gram = gram - below * head
        inverse = jnp.where(row == k, tail, inverse - below * tail)
    diag_ref[...] = diag[:8, :]
    block = block_ref[...].astype(jnp.float32)
    image = jnp.dot(
        inverse, block, precision=lax.Precision.HIGHEST, preferred_element_type=jnp.float32
    )
    out_ref[...] = (image * gain).astype(out_ref.dtype)


def factor(count, gram, block, dtype, gain=1.0):
    height = gram.shape[0]
    vmem = pl.BlockSpec(memory_space=pltpu.VMEM)
    image, diag = pl.pallas_call(
        functools.partial(factor_kernel, count, gain),
        in_specs=[vmem] * 2,
        out_specs=[vmem] * 2,
        out_shape=[
            jax.ShapeDtypeStruct(block.shape, dtype),
            jax.ShapeDtypeStruct((8, height), jnp.float32),
        ],
        name="factor",
    )(gram, block)
    return image, diag[0, :count]


def apply_tile(block, tile, transposed):
    side = 1 if transposed else 0
    product = lax.dot_general(
        block, tile, (((1,), (side,)), ((), ())), preferred_element_type=jnp.float32
    )
    return product.astype(jnp.bfloat16)


def local_gram(block):
    return lax.dot_general(
        block,
        block,
        (((1,), (1,)), ((), ())),
        precision=lax.Precision.HIGHEST,
        preferred_element_type=jnp.float32,
    )


def body(genotypes, snp_index, freq_table, prior, start_vectors):
    allele_freq = jnp.take(freq_table, snp_index)
    standard = standardize(genotypes, allele_freq).astype(jnp.bfloat16)
    row_count = lax.axis_size("row")
    col_count = lax.axis_size("col")
    own_snps = genotypes.shape[0]
    total_snps = own_snps * row_count * col_count
    samples = genotypes.shape[1]
    row_piece = lax.all_to_all(standard, "row", split_axis=1, concat_axis=0, tiled=True)
    col_piece = lax.all_to_all(standard, "col", split_axis=1, concat_axis=0, tiled=True)
    col_panel = lax.all_gather(
        col_piece.reshape(col_count, 1, own_snps, col_piece.shape[1]), "row", axis=1, tiled=True
    ).reshape(total_snps, col_piece.shape[1])
    row_panel = lax.all_gather(row_piece, "col", axis=0, tiled=True)
    grm, tile = make_tile(row_panel, col_panel, prior)

    count = start_vectors.shape[1]
    height = -(-count // 32) * 32
    root = float(samples) ** 0.5
    start = jnp.pad((start_vectors / root).T, ((0, height - count), (0, 0))).astype(jnp.bfloat16)
    diagonals = []
    (image,) = axis_sum("row", 1, apply_tile(start, tile, False))
    for step in range(1, ITERS):
        axis, ident = ("col", 2 * step) if step % 2 == 1 else ("row", 2 * step + 1)
        product, gram = axis_sum(
            axis, ident, apply_tile(image, tile, step % 2 == 1), local_gram(image)
        )
        last = step == ITERS - 1
        image, diag = factor(count, gram, product, jnp.float32 if last else jnp.bfloat16)
        diagonals.append(diag)
    (gram,) = axis_sum("col", 2 * ITERS, None, local_gram(image))
    image, diag = factor(count, gram, image, jnp.float32, root)
    diagonals.append(diag)
    return (grm, image[:count].T, jnp.stack(diagonals, axis=0))


def solution(mesh):
    return jax.shard_map(
        body,
        mesh=mesh,
        in_specs=(P(("row", "col"), None), P(("row", "col")), P(), P("row", "col"), P("row", None)),
        out_specs=(P("row", "col"), P("col", None), P()),
        check_vma=False,
    )
```

time: 455 us -> 269 us (0.59)
  waiting for transfers between devices: 195 us -> 67.2 us
  Pallas kernels: 0 us -> 107 us
  matrix products: 112 us -> 32.5 us
  blocking collectives: 105 us -> 36.5 us
  other arithmetic: 17.4 us -> 4.28 us
    psum x3 -> x0, waiting for transfers between devices: 143 us -> none  [the longest x1 55.9 us: body(): image = lax.psum(apply_tile(grm, scaled_start, True), 'row')]
    pallas_call x0 -> x8, Pallas kernels: none -> 107 us  [the longest x4 53 us: axis_sum(): pl.pallas_call(functools.partial(sum_kernel, axis, n, block is not None,...]
    dot_general x7 -> x6, matrix products: 108 us -> 32.5 us  [the longest x3 28.5 us: apply_tile(): lax.dot_general(block, tile, (((1,), (side,)), ((), ())), preferred_eleme...]
    psum x3 -> x0, blocking collectives: 59.9 us -> none  [the longest x1 28.1 us: body(): lax.psum((apply_tile(grm, image, True), local_gram(image)), 'row')]
    all_gather x2, waiting for transfers between devices: 51.6 us -> 67.2 us  [the longest x1 48.5 us: body(): lax.all_gather(col_piece.reshape(col_count, 1, own_snps, col_piece.shape[...]
    another operation x16 -> x1, other arithmetic: 14.6 us -> 0.59 us  [body(): return (grm, image[:count].T, jnp.stack(diagonals, axis=0))]
    all_to_all x1, blocking collectives: 31.8 us -> 21.6 us  [body(): lax.all_to_all(standard, 'row', split_axis=1, concat_axis=0, tiled=True)]
    all_gather x1 -> x0, local copies, waits for them, and re-layouts: 6.46 us -> none  [body(): col_panel = lax.all_gather(col_piece, 'row', axis=1, tiled=True)]
  transfers between devices with their start and end apart: 5 -> 2, of which waited for: 5 -> 2; matrix products, arithmetic and copies ran while one was open for 3% -> 0% of each run, Pallas kernels for 0% -> 0%
where the time goes in v1:
time: 269 us; the launch traced here: 268 us
  Pallas kernels  107 us (40%)
  waiting for transfers between devices  67.2 us (25%)
  blocking collectives  36.5 us (14%)
  matrix products  32.5 us (12%)
  between operations  14.1 us (5%)
  local copies, waits for them, and re-layouts  6.7 us (2%)
  other arithmetic  4.28 us (2%)
    pallas_call x4, Pallas kernels, axis_sum(): pl.pallas_call(functools.partial(sum_kernel, axis, n, block is not None,...  53 us
    all_gather x1, waiting for transfers between devices, body(): lax.all_gather(col_piece.reshape(col_count, 1, own_snps, col_piece.shape[...  48.5 us
    pallas_call x1, Pallas kernels, make_tile(): pl.pallas_call(functools.partial(tile_kernel, 1.0 / depth), grid=(rows //...  41.3 us
    dot_general x3, matrix products, apply_tile(): lax.dot_general(block, tile, (((1,), (side,)), ((), ())), preferred_eleme...  28.5 us
    all_to_all x1, blocking collectives, body(): lax.all_to_all(standard, 'row', split_axis=1, concat_axis=0, tiled=True)  21.6 us
    all_gather x1, waiting for transfers between devices, body(): row_panel = lax.all_gather(row_piece, 'col', axis=0, tiled=True)  18.7 us
    all_to_all x1, blocking collectives, body(): lax.all_to_all(standard, 'col', split_axis=1, concat_axis=0, tiled=True)  14.9 us
    pallas_call x3, Pallas kernels, factor(): pl.pallas_call(functools.partial(factor_kernel, count, gain), in_specs=[v...  12.4 us
  transfers between devices with their start and end apart: 2, of which 2 were waited for; matrix products, arithmetic and copies ran while one was open for 0% of the time, Pallas kernels for 0%

profile of v1, /device:TPU:0, one launch (start us, length us, event | category | flops | bytes accessed | tf_op | source)
XLA Modules:
  0.0 268.1 jit_solution(11374548796457651977)
XLA Ops:
  7.2 0.0 copy-start
  7.2 0.0 all-gather.4.cloned.1.call-start
  7.2 0.7 compare_select_fusion
  7.9 0.0 copy-done
  7.9 0.7 gather_fusion
  8.6 0.7 broadcast_multiply_fusion
  9.2 1.4 divide_convert_fusion
  10.7 21.6 %all_to_all.35 = bf16[16,8,2048]{2,0,1:T(8,128)(2,1)} all-to-all(bf16[16,8,2048]{2,0,1:T(8,128)(2,1)S(1)} %bitcast.55), channel_id=1, replica_groups=mesh['row'=8,'col'=4] {'row'}, dimensions={1} | all-to-all | bytes 1048576 | tf_op jit(solution)/shard_map/all_to_all | solution.py:224
  32.3 0.0 all-gather.4.cloned.1.call-update
  32.3 0.0 all-gather.6.cloned.1.call-start
  32.4 14.9 %all_to_all.36 = bf16[16,4,4096]{2,0,1:T(8,128)(2,1)} all-to-all(bf16[16,4,4096]{2,0,1:T(8,128)(2,1)S(1)} %bitcast.54), channel_id=1, replica_groups=mesh['row'=8,'col'=4] {'col'}, dimensions={1} | all-to-all | bytes 1048576 | tf_op jit(solution)/shard_map/all_to_all | solution.py:225
  47.3 0.0 all-gather.6.cloned.1.call-update
  47.3 0.9 fusion.1
  48.2 18.7 %all-gather.4.cloned.1.call-done.rows_ref = bf16[512,2048]{1,0:T(8,128)(2,1)} async-done(((bf16[128,2048]{1,0:T(8,128)(2,1)}), bf16[512,2048]{1,0:T(8,128)(2,1)}) %all-gather.4.cloned.1.call-update) | async-done | bytes 2097168 | tf_op jit(solution)/shard_map/all_gather | solution.py:229
  66.9 48.5 %all-gather.6.cloned.1.call-done = bf16[4,128,4096]{2,1,0:T(8,128)(2,1)} async-done(((bf16[4,16,4096]{2,1,0:T(8,128)(2,1)}), bf16[4,128,4096]{2,1,0:T(8,128)(2,1)}) %all-gather.6.cloned.1.call-update) | async-done | bytes 4194320 | tf_op jit(solution)/shard_map/all_gather | solution.py:226
  115.4 41.3 %tile.1 = (f32[2048,4096]{1,0:T(8,128)}, bf16[2048,4096]{1,0:T(8,128)(2,1)}) custom-call(bf16[512,2048]{1,0:T(8,128)(2,1)} %all-gather.4.cloned.1.call-done.rows_ref, bf16[512,4096]{1,0:T(8,128)(2,1)} %bitcast.51, f32[2048,4096]{1,0:T(8,128)} %prior_ref.1), custom_call_target="tpu_custom_call" | custom-call | flops 8589934592 | bytes 83886080 | tf_op jit(solution)/shard_map/tile/pallas_call | solution.py:35
  156.7 8.8 %convolution_convert_fusion.1 = bf16[32,4096]{1,0:T(8,128)(2,1)S(1)} fusion(bf16[2048,4096]{1,0:T(8,128)(2,1)} %get-tuple-element.16, bf16[20,2048]{1,0:T(8,128)(2,1)S(1)} %fusion.1), kind=kOutput, calls=%fused_computation.2 | convolution fusion | flops 537001984 | bytes 17121280 | tf_op jit(solution)/shard_map/dot_general | solution.py:200
  165.5 0.7 copy.28
  166.2 15.5 %sum1.1 = bf16[32,4096]{1,0:T(8,128)(2,1)} custom-call(bf16[8,32,512]{2,1,0:T(8,128)(2,1)} %bitcast.59), custom_call_target="tpu_custom_call" | custom-call | tf_op jit(solution)/shard_map/sum1/pallas_call | solution.py:147
  181.7 0.0 copy-start.2
  181.7 0.0 copy-start.1
  181.8 10.9 %convolution_convert_fusion.2 = bf16[32,2048]{1,0:T(8,128)(2,1)S(1)} fusion(bf16[32,4096]{1,0:T(8,128)(2,1)} %sum1.1, bf16[2048,4096]{1,0:T(8,128)(2,1)} %get-tuple-element.16), kind=kOutput, calls=%fused_computation.3 | convolution fusion | flops 536936448 | bytes 17170432 | tf_op jit(solution)/shard_map/dot_general | solution.py:200
  192.7 0.0 copy-done.2
  192.7 0.8 fusion.3.refs_1_
  193.5 0.7 copy.29
  194.2 11.9 %sum2.1 = (bf16[32,2048]{1,0:T(8,128)(2,1)}, f32[32,32]{1,0:T(8,128)}) custom-call(bf16[4,32,512]{2,1,0:T(8,128)(2,1)} %bitcast.61, f32[32,32]{1,0:T(8,128)} %fusion.3.refs_1_), custom_call_target="tpu_custom_call" | custom-call | tf_op jit(solution)/shard_map/sum2/pallas_call | solution.py:147
  206.1 3.9 %factor.3 = (bf16[32,2048]{1,0:T(8,128)(2,1)}, f32[8,32]{1,0:T(8,128)}) custom-call(f32[32,32]{1,0:T(8,128)} %get-tuple-element.17.gram_ref, bf16[32,2048]{1,0:T(8,128)(2,1)} %get-tuple-element.18.block_ref), custom_call_target="tpu_custom_call" | custom-call | tf_op jit(solution)/shard_map/factor/pallas_call | solution.py:185
  209.9 0.0 copy-start.3
  209.9 8.9 %convolution_convert_fusion = bf16[32,4096]{1,0:T(8,128)(2,1)S(1)} fusion(bf16[32,2048]{1,0:T(8,128)(2,1)} %get-tuple-element.19, bf16[2048,4096]{1,0:T(8,128)(2,1)} %get-tuple-element.16), kind=kOutput, calls=%fused_computation.1 | convolution fusion | flops 537001984 | bytes 17170432 | tf_op jit(solution)/shard_map/dot_general | solution.py:200
  218.8 0.0 copy-done.3
  218.8 0.8 fusion.4.refs_1_
  219.6 0.7 copy.27
  220.3 19.6 %sum5.1 = (bf16[32,4096]{1,0:T(8,128)(2,1)}, f32[32,32]{1,0:T(8,128)}) custom-call(bf16[8,32,512]{2,1,0:T(8,128)(2,1)} %bitcast.58, f32[32,32]{1,0:T(8,128)} %fusion.4.refs_1_), custom_call_target="tpu_custom_call" | custom-call | tf_op jit(solution)/shard_map/sum5/pallas_call | solution.py:147
  239.9 4.2 %factor.4 = (f32[32,4096]{1,0:T(8,128)}, f32[8,32]{1,0:T(8,128)}) custom-call(f32[32,32]{1,0:T(8,128)} %get-tuple-element.20.gram_ref, bf16[32,4096]{1,0:T(8,128)(2,1)} %get-tuple-element.21.block_ref), custom_call_target="tpu_custom_call" | custom-call | tf_op jit(solution)/shard_map/factor/pallas_call | solution.py:185
  244.1 2.4 fusion.5.refs_0_
  246.5 6.0 %sum6.1.gram_ref = f32[32,32]{1,0:T(8,128)} custom-call(f32[32,32]{1,0:T(8,128)} %fusion.5.refs_0_), custom_call_target="tpu_custom_call" | custom-call | tf_op jit(solution)/shard_map/sum6/pallas_call | solution.py:147
  252.5 4.3 %factor.5 = (f32[32,4096]{1,0:T(8,128)}, f32[8,32]{1,0:T(8,128)}) custom-call(f32[32,32]{1,0:T(8,128)} %sum6.1.gram_ref, f32[32,4096]{1,0:T(8,128)} %get-tuple-element.22.block_ref), custom_call_target="tpu_custom_call" | custom-call | tf_op jit(solution)/shard_map/factor/pallas_call | solution.py:185
  256.9 0.7 slice.15
  257.6 0.7 slice.14
  258.2 0.7 slice.13
  258.9 1.8 slice_bitcast_fusion
  260.7 0.6 pad_maximum_fusion
  261.3 0.0 copy-done.1
  (4 shorter events, 0.1 us)
Async XLA Ops:
  7.2 0.7 copy-start
  7.2 59.7 %all-gather.4.cloned.1.call-start = ((), (), s32[]{:S(2)}) async-start(), calls=%async_computation.2 | async-start | bytes 2621440 | tf_op jit(solution)/shard_map/all_gather | solution.py:229
  32.3 83.1 %all-gather.6.cloned.1.call-start = ((), (), s32[]{:S(2)}) async-start(), calls=%async_computation.3 | async-start | bytes 4718592 | tf_op jit(solution)/shard_map/all_gather | solution.py:226
  181.7 11.0 %copy-start.2 = (bf16[32,4096]{1,0:T(8,128)(2,1)S(1)}, bf16[32,4096]{1,0:T(8,128)(2,1)}, u32[]{:S(2)}) copy-start(bf16[32,4096]{1,0:T(8,128)(2,1)} %sum1.1) | copy-start | bytes 786436
  181.7 79.5 %copy-start.1 = (f32[2048]{0:T(1024)S(1)}, f32[2048]{0:T(1024)}, u32[]{:S(2)}) copy-start(f32[2048]{0:T(1024)} %param.7) | copy-start | bytes 24580
  209.9 8.9 %copy-start.3 = (bf16[32,2048]{1,0:T(8,128)(2,1)S(1)}, bf16[32,2048]{1,0:T(8,128)(2,1)}, u32[]{:S(2)}) copy-start(bf16[32,2048]{1,0:T(8,128)(2,1)} %get-tuple-element.19) | copy-start | bytes 393220
Sparse Core Ops, SparseCore 0:
  32.4 34.4 all-gather.3
  68.5 46.8 all-gather.5
